TPU v7x, 32 devices: a whole 2x2x4 slice. The times are simulated.
32 devices in a mesh: dp: 8 (over y, x, core), seq: 4 (over z).
Axes of the slice: x: 2, y: 2, z: 4, core: 2. Of those that a mesh axis runs over, the one named last changes fastest.
Arguments:
- img_q_raw: bfloat16 [8, 512, 1536], P('dp', 'seq'), may hold values from -12 to 12
- img_k_raw: bfloat16 [8, 512, 1536], P('dp', 'seq'), may hold values from -6 to 6
- img_v: bfloat16 [8, 512, 1536], P('dp', 'seq'), may hold values from -6 to 6
- img_dout: bfloat16 [8, 512, 1536], P('dp', 'seq'), may hold values from -6 to 6
- txt_q_raw: bfloat16 [8, 64, 1536], P('dp', 'seq'), may hold values from -6 to 6
- txt_k_raw: bfloat16 [8, 64, 1536], P('dp'), may hold values from -6 to 6
- txt_v: bfloat16 [8, 64, 1536], P('dp'), may hold values from -6 to 6
- txt_dout: bfloat16 [8, 64, 1536], P('dp', 'seq'), may hold values from -6 to 6
- q_gain: float32 [128], replicated, may hold values from 0.6 to 3.8
- k_gain: float32 [128], replicated, may hold values from 0.6 to 3.8
Outputs:
- img_dq: bfloat16 [8, 512, 1536], P('dp', 'seq')
- img_dk: bfloat16 [8, 512, 1536], P('dp', 'seq')
- img_dv: bfloat16 [8, 512, 1536], P('dp', 'seq')
- txt_dq: bfloat16 [8, 64, 1536], P('dp', 'seq')
- txt_dk: bfloat16 [8, 64, 1536], P('dp', 'seq')
- txt_dv: bfloat16 [8, 64, 1536], P('dp', 'seq')
- q_gain_grad: float32 [128], replicated
- k_gain_grad: float32 [128], replicated
All inputs are finite; a program needn't handle non-finite values.
Results may differ from a plain program's by a relative error of at most 0.012.
The roundings to bfloat16 on the way count: a program that leaves them out, or rounds other values in their place, can miss the bound.
Values may be sent and summed in bfloat16 or wider, within the bound.
A program may use at most 64 MiB of HBM per device.

v0:
```python
import jax
import jax.numpy as jnp
from jax import lax
from jax.sharding import PartitionSpec as P

HEAD_DIM = 128
epsilon = 1e-06


def normalize(source, norm_gain):
    values = source.astype(jnp.float32)
    inverse = lax.rsqrt(jnp.mean(values * values, axis=-1, keepdims=True) + epsilon)
    return values * inverse * norm_gain


def norm_backward(source, norm_gain, upstream):
    values = source.astype(jnp.float32)
    result_value, pullback = jax.vjp(normalize, values, norm_gain)
    return pullback(upstream)


def group_back(operands):
    query_b, key_b, value_all, dout_blocks = operands
    score_scale = query_b.shape[-1] ** (-0.5)
    scores = (
        jnp.einsum("nqhd,khd->nhqk", query_b, key_b, preferred_element_type=jnp.float32)
        * score_scale
    )
    row_max = jnp.max(scores, axis=-1, keepdims=True)
    shifted = scores - row_max
    log_total = jnp.log(jnp.sum(jnp.exp(shifted), axis=-1, keepdims=True))
    prob_full = jnp.exp(shifted - log_total)
    probs_b = prob_full.astype(jnp.bfloat16)
    output_b = jnp.einsum(
        "nhqk,khd->nqhd", probs_b, value_all, preferred_element_type=jnp.float32
    ).astype(jnp.bfloat16)
    output_b = lax.optimization_barrier(output_b)
    dprob = jnp.einsum("nqhd,khd->nhqk", dout_blocks, value_all, preferred_element_type=jnp.float32)
    row_delta = jnp.sum(dout_blocks.astype(jnp.float32) * output_b.astype(jnp.float32), axis=-1)
    row_delta = jnp.transpose(row_delta, (0, 2, 1))[..., None]
    dscore_b = (prob_full * (dprob - row_delta) * score_scale).astype(jnp.bfloat16)
    dquery = jnp.einsum("nhqk,khd->nqhd", dscore_b, key_b, preferred_element_type=jnp.float32)
    key_terms = jnp.einsum("nhqk,nqhd->nkhd", dscore_b, query_b, preferred_element_type=jnp.float32)
    value_terms = jnp.einsum(
        "nhqk,nqhd->nkhd", probs_b, dout_blocks, preferred_element_type=jnp.float32
    )
    return (dquery, key_terms, value_terms)


def forward_back(query_b, key_b, value_all, dout_blocks):
    block_count, query_rows, heads_here, feature_count = query_b.shape
    key_rows = key_b.shape[0]
    group_count = heads_here // heads_here

    def split_rows(source):
        return jnp.moveaxis(
            source.reshape(block_count, query_rows, group_count, heads_here, feature_count), 2, 0
        )

    def split_keys(source):
        return jnp.moveaxis(source.reshape(key_rows, group_count, heads_here, feature_count), 1, 0)

    dquery_g, key_g, value_g = lax.map(
        group_back,
        (split_rows(query_b), split_keys(key_b), split_keys(value_all), split_rows(dout_blocks)),
    )
    dquery = jnp.moveaxis(dquery_g, 0, 2).reshape(
        block_count, query_rows, heads_here, feature_count
    )
    key_terms = jnp.moveaxis(key_g, 0, 2).reshape(block_count, key_rows, heads_here, feature_count)
    value_terms = jnp.moveaxis(value_g, 0, 2).reshape(
        block_count, key_rows, heads_here, feature_count
    )
    return (dquery, key_terms, value_terms)


def local(
    img_q_raw, img_k_raw, img_v, img_dout, txt_q_raw, txt_k_raw, txt_v, txt_dout, q_gain, k_gain
):
    seq_count = lax.axis_size("seq")
    my_index = lax.axis_index("seq")
    image_q = img_q_raw[0]
    image_k = img_k_raw[0]
    image_v = img_v[0]
    image_d = img_dout[0]
    text_q = txt_q_raw[0]
    text_k = txt_k_raw[0]
    text_v = txt_v[0]
    text_d = txt_dout[0]
    lane_width = image_q.shape[1]
    head_count = lane_width // HEAD_DIM
    img_rows = image_q.shape[0]
    text_rows = text_q.shape[0]
    text_all = text_k.shape[0]
    image_total = img_rows * seq_count
    exchanged = (
        lax.all_to_all(image_q, "seq", split_axis=1, concat_axis=0, tiled=True),
        lax.all_to_all(image_k, "seq", split_axis=1, concat_axis=0, tiled=True),
        lax.all_to_all(image_v, "seq", split_axis=1, concat_axis=0, tiled=True),
        lax.all_to_all(image_d, "seq", split_axis=1, concat_axis=0, tiled=True),
        lax.all_to_all(text_q, "seq", split_axis=1, concat_axis=0, tiled=True),
        lax.all_to_all(text_d, "seq", split_axis=1, concat_axis=0, tiled=True),
    )
    moved_iq, moved_ik, moved_iv, moved_id, moved_tq, moved_td = exchanged
    local_heads = head_count // seq_count
    head_lanes = local_heads * HEAD_DIM
    key_text = lax.dynamic_slice_in_dim(text_k, my_index * head_lanes, head_lanes, 1)
    value_text = lax.dynamic_slice_in_dim(text_v, my_index * head_lanes, head_lanes, 1)
    query_src = jnp.concatenate(
        [
            moved_iq.reshape(seq_count, img_rows, local_heads, HEAD_DIM),
            moved_tq.reshape(seq_count, text_rows, local_heads, HEAD_DIM),
        ],
        axis=1,
    )
    dout_blocks = jnp.concatenate(
        [
            moved_id.reshape(seq_count, img_rows, local_heads, HEAD_DIM),
            moved_td.reshape(seq_count, text_rows, local_heads, HEAD_DIM),
        ],
        axis=1,
    )
    key_src = jnp.concatenate([moved_ik, key_text], axis=0).reshape(
        image_total + text_all, local_heads, HEAD_DIM
    )
    value_all = jnp.concatenate([moved_iv, value_text], axis=0).reshape(
        image_total + text_all, local_heads, HEAD_DIM
    )
    query_b = normalize(query_src, q_gain).astype(jnp.bfloat16)
    key_b = normalize(key_src, k_gain).astype(jnp.bfloat16)
    dquery, key_f, value_f = forward_back(query_b, key_b, value_all, dout_blocks)
    key_terms = key_f.astype(jnp.bfloat16)
    value_terms = value_f.astype(jnp.bfloat16)
    key_terms, value_terms = lax.optimization_barrier((key_terms, value_terms))
    dkey = jnp.sum(key_terms.astype(jnp.float32), axis=0)
    dvalue = jnp.sum(value_terms.astype(jnp.float32), axis=0)
    dquery_src, dq_gain = norm_backward(query_src, q_gain, dquery)
    dkey_src, dk_gain = norm_backward(key_src, k_gain, dkey)
    dq_b = dquery_src.astype(jnp.bfloat16)
    dk_b = dkey_src.reshape(image_total + text_all, head_lanes).astype(jnp.bfloat16)
    dv_b = dvalue.reshape(image_total + text_all, head_lanes).astype(jnp.bfloat16)
    returned = (
        dq_b[:, :img_rows].reshape(image_total, head_lanes),
        dk_b[:image_total],
        dv_b[:image_total],
        dq_b[:, img_rows:].reshape(text_all, head_lanes),
        dk_b[image_total:],
        dv_b[image_total:],
    )
    grad_iq, grad_ik, grad_iv, grad_tq, grad_tk, grad_tv = (
        lax.all_to_all(returned[0], "seq", split_axis=0, concat_axis=1, tiled=True),
        lax.all_to_all(returned[1], "seq", split_axis=0, concat_axis=1, tiled=True),
        lax.all_to_all(returned[2], "seq", split_axis=0, concat_axis=1, tiled=True),
        lax.all_to_all(returned[3], "seq", split_axis=0, concat_axis=1, tiled=True),
        lax.all_to_all(returned[4], "seq", split_axis=0, concat_axis=1, tiled=True),
        lax.all_to_all(returned[5], "seq", split_axis=0, concat_axis=1, tiled=True),
    )
    gain_q, gain_k = lax.psum((dq_gain, dk_gain), ("dp", "seq"))
    return (
        grad_iq[None],
        grad_ik[None],
        grad_iv[None],
        grad_tq[None],
        grad_tk[None],
        grad_tv[None],
        gain_q,
        gain_k,
    )


def solution(mesh):
    return jax.shard_map(
        local,
        mesh=mesh,
        in_specs=(
            P("dp", "seq", None),
            P("dp", "seq", None),
            P("dp", "seq", None),
            P("dp", "seq", None),
            P("dp", "seq", None),
            P("dp", None, None),
            P("dp", None, None),
            P("dp", "seq", None),
            P(),
            P(),
        ),
        out_specs=(
            P("dp", "seq", None),
            P("dp", "seq", None),
            P("dp", "seq", None),
            P("dp", "seq", None),
            P("dp", "seq", None),
            P("dp", "seq", None),
            P(),
            P(),
        ),
        check_vma=False,
    )
```

profile of v0, /device:TPU:0, one launch (start us, length us, event | category | flops | bytes accessed | tf_op | source)
XLA Modules:
  0.0 206.6 jit_solution(5955745471128264303)
XLA Ops:
  2.2 6.3 %all-to-all-start.2 = ((bf16[16,4,384]{2,0,1:T(8,128)(2,1)}), bf16[16,4,384]{2,0,1:T(8,128)(2,1)S(1)}, u32[]{:S(2)}, u32[]{:S(2)}) async-start(bf16[16,4,384]{2,0,1:T(8,128)(2,1)} %copy.91), calls=%async_computation.2 | async-start | bytes 98304 | tf_op jit(solution)/shard_map/all_to_all | solution.py:101
  9.9 4.3 %all-to-all-done.2 = bf16[16,4,384]{2,0,1:T(8,128)(2,1)S(1)} async-done(((bf16[16,4,384]{2,0,1:T(8,128)(2,1)}), bf16[16,4,384]{2,0,1:T(8,128)(2,1)S(1)}, u32[]{:S(2)}, u32[]{:S(2)}) %all-to-all-start.2) | async-done | bytes 49184 | tf_op jit(solution)/shard_map/all_to_all | solution.py:101
  14.2 3.3 %all-to-all-start.5 = ((bf16[16,4,384]{2,0,1:T(8,128)(2,1)}), bf16[16,4,384]{2,0,1:T(8,128)(2,1)S(1)}, u32[]{:S(2)}, u32[]{:S(2)}) async-start(bf16[16,4,384]{2,0,1:T(8,128)(2,1)} %copy.99), calls=%async_computation.5 | async-start | bytes 98304 | tf_op jit(solution)/shard_map/all_to_all | solution.py:102
  19.4 3.8 %all-to-all-done.5 = bf16[16,4,384]{2,0,1:T(8,128)(2,1)S(1)} async-done(((bf16[16,4,384]{2,0,1:T(8,128)(2,1)}), bf16[16,4,384]{2,0,1:T(8,128)(2,1)S(1)}, u32[]{:S(2)}, u32[]{:S(2)}) %all-to-all-start.5) | async-done | bytes 49184 | tf_op jit(solution)/shard_map/all_to_all | solution.py:102
  23.1 3.5 %all-to-all-start = ((bf16[128,4,384]{0,2,1:T(8,128)(2,1)}), bf16[128,4,384]{0,2,1:T(8,128)(2,1)S(1)}, u32[]{:S(2)}, u32[]{:S(2)}) async-start(bf16[128,4,384]{0,2,1:T(8,128)(2,1)} %bitcast), calls=%async_computation | async-start | bytes 786432 | tf_op jit(solution)/shard_map/all_to_all | solution.py:98
  36.0 3.5 %all-to-all-start.1 = ((bf16[128,4,384]{0,2,1:T(8,128)(2,1)}), bf16[128,4,384]{0,2,1:T(8,128)(2,1)S(1)}, u32[]{:S(2)}, u32[]{:S(2)}) async-start(bf16[128,4,384]{0,2,1:T(8,128)(2,1)} %bitcast.4), calls=%async_computation.1 | async-start | bytes 786432 | tf_op jit(solution)/shard_map/all_to_all | solution.py:97
  40.2 8.6 %all-to-all-done.1 = bf16[128,4,384]{0,2,1:T(8,128)(2,1)S(1)} async-done(((bf16[128,4,384]{0,2,1:T(8,128)(2,1)}), bf16[128,4,384]{0,2,1:T(8,128)(2,1)S(1)}, u32[]{:S(2)}, u32[]{:S(2)}) %all-to-all-start.1) | async-done | bytes 393248 | tf_op jit(solution)/shard_map/all_to_all | solution.py:97
  48.7 3.5 %all-to-all-start.3 = ((bf16[128,4,384]{0,2,1:T(8,128)(2,1)}), bf16[128,4,384]{0,2,1:T(8,128)(2,1)S(1)}, u32[]{:S(2)}, u32[]{:S(2)}) async-start(bf16[128,4,384]{0,2,1:T(8,128)(2,1)} %bitcast.12), calls=%async_computation.3 | async-start | bytes 786432 | tf_op jit(solution)/shard_map/all_to_all | solution.py:99
  54.5 2.9 %fusion.39 = f32[3,576,576]{1,2,0} fusion(bf16[3,128,576]{1,2,0:T(8,128)(2,1)S(1)} %bitcast.111, f32[128]{0:T(128)S(1)} %copy-done.15, f32[576,3]{0,1:T(4,128)S(1)} %fusion.43, bf16[64,3,128]{2,0,1:T(8,128)(2,1)S(1)} %copy.89, bf16[512,3,128]{2,0,1:T(8,128)(2,1)S(1)} %copy.88), kind=kOutput, calls=%fused_computation.57 | convolution fusion | flops 256352256 | bytes 4873472
  57.3 4.2 %all-to-all-done.3 = bf16[128,4,384]{0,2,1:T(8,128)(2,1)S(1)} async-done(((bf16[128,4,384]{0,2,1:T(8,128)(2,1)}), bf16[128,4,384]{0,2,1:T(8,128)(2,1)S(1)}, u32[]{:S(2)}, u32[]{:S(2)}) %all-to-all-start.3) | async-done | bytes 393248 | tf_op jit(solution)/shard_map/all_to_all | solution.py:99
  61.5 3.6 %all-to-all-start.4 = ((bf16[128,4,384]{0,2,1:T(8,128)(2,1)}), bf16[128,4,384]{0,2,1:T(8,128)(2,1)S(1)}, u32[]{:S(2)}, u32[]{:S(2)}) async-start(bf16[128,4,384]{0,2,1:T(8,128)(2,1)} %bitcast.14), calls=%async_computation.4 | async-start | bytes 786432 | tf_op jit(solution)/shard_map/all_to_all | solution.py:100
  65.2 6.4 %bitcast_subtract_fusion = f32[4,3,144,576]{3,2,0,1:T(8,128)} fusion(f32[3,576,4,144]{1,3,2,0:T(8,128)} %bitcast.107), kind=kOutput, calls=%fused_computation.5 | output fusion | flops 2988287 | bytes 7962624 | tf_op jit(solution)/shard_map/while/body/eval_jaxpr/sub | solution.py:30
  72.9 7.0 %fusion.47 = (bf16[4,3,144,576]{3,2,0,1:T(8,128)(2,1)S(1)}, f32[4,3,144,576]{3,2,0,1:T(8,128)}) fusion(f32[4,3,144,576]{3,2,0,1:T(8,128)} %bitcast_subtract_fusion), kind=kOutput, calls=%fused_computation.75 | output fusion | flops 1992959 | bytes 9953280 | tf_op jit(solution)/shard_map/while/body/eval_jaxpr/reduce_sum | solution.py:31
  98.4 4.9 %all-to-all-start.10 = ((bf16[4,16,384]{2,1,0:T(8,128)(2,1)}), bf16[4,16,384]{2,1,0:T(8,128)(2,1)S(1)}, u32[]{:S(2)}, u32[]{:S(2)}) async-start(bf16[4,16,384]{2,1,0:T(8,128)(2,1)} %bitcast.44), calls=%async_computation.10 | async-start | bytes 98304 | tf_op jit(solution)/shard_map/all_to_all | solution.py:155
  109.0 3.5 %all-to-all-start.11 = ((bf16[4,16,384]{2,1,0:T(8,128)(2,1)}), bf16[4,16,384]{2,1,0:T(8,128)(2,1)S(1)}, u32[]{:S(2)}, u32[]{:S(2)}) async-start(bf16[4,16,384]{2,1,0:T(8,128)(2,1)} %all_to_all.177), calls=%async_computation.11 | async-start | bytes 98304 | tf_op jit(solution)/shard_map/all_to_all | solution.py:156
  113.2 5.0 %all-to-all-done.11 = bf16[4,16,384]{2,1,0:T(8,128)(2,1)S(1)} async-done(((bf16[4,16,384]{2,1,0:T(8,128)(2,1)}), bf16[4,16,384]{2,1,0:T(8,128)(2,1)S(1)}, u32[]{:S(2)}, u32[]{:S(2)}) %all-to-all-start.11) | async-done | bytes 49184 | tf_op jit(solution)/shard_map/all_to_all | solution.py:156
  118.2 3.3 %all-to-all-start.9 = ((bf16[4,16,384]{2,1,0:T(8,128)(2,1)}), bf16[4,16,384]{2,1,0:T(8,128)(2,1)S(1)}, u32[]{:S(2)}, u32[]{:S(2)}) async-start(bf16[4,16,384]{2,1,0:T(8,128)(2,1)} %copy_bitcast_fusion), calls=%async_computation.9 | async-start | bytes 98304 | tf_op jit(solution)/shard_map/all_to_all | solution.py:154
  122.4 4.8 %all-to-all-done.9 = bf16[4,16,384]{2,1,0:T(8,128)(2,1)S(1)} async-done(((bf16[4,16,384]{2,1,0:T(8,128)(2,1)}), bf16[4,16,384]{2,1,0:T(8,128)(2,1)S(1)}, u32[]{:S(2)}, u32[]{:S(2)}) %all-to-all-start.9) | async-done | bytes 49184 | tf_op jit(solution)/shard_map/all_to_all | solution.py:154
  127.2 3.5 %all-to-all-start.7 = ((bf16[4,128,384]{2,1,0:T(8,128)(2,1)}), bf16[4,128,384]{2,1,0:T(8,128)(2,1)S(1)}, u32[]{:S(2)}, u32[]{:S(2)}) async-start(bf16[4,128,384]{2,1,0:T(8,128)(2,1)} %bitcast.38), calls=%async_computation.7 | async-start | bytes 786432 | tf_op jit(solution)/shard_map/all_to_all | solution.py:152
  131.8 7.7 %all-to-all-done.7 = bf16[4,128,384]{2,1,0:T(8,128)(2,1)S(1)} async-done(((bf16[4,128,384]{2,1,0:T(8,128)(2,1)}), bf16[4,128,384]{2,1,0:T(8,128)(2,1)S(1)}, u32[]{:S(2)}, u32[]{:S(2)}) %all-to-all-start.7) | async-done | bytes 393248 | tf_op jit(solution)/shard_map/all_to_all | solution.py:152
  139.6 5.6 %all-to-all-start.8 = ((bf16[4,128,384]{1,2,0:T(8,128)(2,1)}), bf16[4,128,384]{1,2,0:T(8,128)(2,1)S(1)}, u32[]{:S(2)}, u32[]{:S(2)}) async-start(bf16[4,128,384]{1,2,0:T(8,128)(2,1)} %copy.115), calls=%async_computation.8 | async-start | bytes 786432 | tf_op jit(solution)/shard_map/all_to_all | solution.py:153
  146.1 11.2 %all-to-all-done.8 = bf16[4,128,384]{1,2,0:T(8,128)(2,1)S(1)} async-done(((bf16[4,128,384]{1,2,0:T(8,128)(2,1)}), bf16[4,128,384]{1,2,0:T(8,128)(2,1)S(1)}, u32[]{:S(2)}, u32[]{:S(2)}) %all-to-all-start.8) | async-done | bytes 393248 | tf_op jit(solution)/shard_map/all_to_all | solution.py:153
  157.4 3.5 %all-to-all-start.6 = ((bf16[4,128,384]{1,2,0:T(8,128)(2,1)}), bf16[4,128,384]{1,2,0:T(8,128)(2,1)S(1)}, u32[]{:S(2)}, u32[]{:S(2)}) async-start(bf16[4,128,384]{1,2,0:T(8,128)(2,1)} %bitcast.27), calls=%async_computation.6 | async-start | bytes 786432 | tf_op jit(solution)/shard_map/all_to_all | solution.py:151
  160.8 40.7 %all-reduce = (f32[128]{0:T(128)}, f32[128]{0:T(128)}) all-reduce(f32[128]{0:T(128)S(1)} %copy-done.20, f32[128]{0:T(128)S(1)} %copy-done.19), channel_id=1, replica_groups=mesh['dp'=8,'seq'=4] {'dp','seq'}, use_global_device_ids=true, to_apply=%region_10.11 | all-reduce | flops 256 | bytes 2048 | tf_op jit(solution)/shard_map/psum | solution.py:158
  (123 shorter events, 51.1 us)
Async XLA Ops:
  0.6 32.1 %copy-start.7 = (bf16[1,128,1536]{2,1,0:T(8,128)(2,1)S(1)}, bf16[1,128,1536]{2,1,0:T(8,128)(2,1)}, u32[]{:S(2)}) copy-start(bf16[1,128,1536]{2,1,0:T(8,128)(2,1)} %param.13) | copy-start | bytes 1179652
  0.6 38.8 %copy-start.15 = (f32[128]{0:T(128)S(1)}, f32[128]{0:T(128)}, u32[]{:S(2)}) copy-start(f32[128]{0:T(128)} %param.19) | copy-start | bytes 1540
  2.2 12.0 %all-to-all-start.2 = ((bf16[16,4,384]{2,0,1:T(8,128)(2,1)}), bf16[16,4,384]{2,0,1:T(8,128)(2,1)S(1)}, u32[]{:S(2)}, u32[]{:S(2)}) async-start(bf16[16,4,384]{2,0,1:T(8,128)(2,1)} %copy.91), calls=%async_computation.2 | async-start | bytes 98304 | tf_op jit(solution)/shard_map/all_to_all | solution.py:101
  14.2 8.9 %all-to-all-start.5 = ((bf16[16,4,384]{2,0,1:T(8,128)(2,1)}), bf16[16,4,384]{2,0,1:T(8,128)(2,1)S(1)}, u32[]{:S(2)}, u32[]{:S(2)}) async-start(bf16[16,4,384]{2,0,1:T(8,128)(2,1)} %copy.99), calls=%async_computation.5 | async-start | bytes 98304 | tf_op jit(solution)/shard_map/all_to_all | solution.py:102
  23.1 12.8 %all-to-all-start = ((bf16[128,4,384]{0,2,1:T(8,128)(2,1)}), bf16[128,4,384]{0,2,1:T(8,128)(2,1)S(1)}, u32[]{:S(2)}, u32[]{:S(2)}) async-start(bf16[128,4,384]{0,2,1:T(8,128)(2,1)} %bitcast), calls=%async_computation | async-start | bytes 786432 | tf_op jit(solution)/shard_map/all_to_all | solution.py:98
  27.5 25.9 %copy-start.17 = (f32[128]{0:T(128)S(1)}, f32[128]{0:T(128)}, u32[]{:S(2)}) copy-start(f32[128]{0:T(128)} %param.18) | copy-start | bytes 1540
  36.0 16.3 %copy-start.3 = (bf16[128,4,384]{0,2,1:T(8,128)(2,1)}, bf16[128,4,384]{0,2,1:T(8,128)(2,1)S(1)}, u32[]{:S(2)}) copy-start(bf16[128,4,384]{0,2,1:T(8,128)(2,1)S(1)} %all-to-all-done) | copy-start | bytes 1179652
  36.0 12.8 %all-to-all-start.1 = ((bf16[128,4,384]{0,2,1:T(8,128)(2,1)}), bf16[128,4,384]{0,2,1:T(8,128)(2,1)S(1)}, u32[]{:S(2)}, u32[]{:S(2)}) async-start(bf16[128,4,384]{0,2,1:T(8,128)(2,1)} %bitcast.4), calls=%async_computation.1 | async-start | bytes 786432 | tf_op jit(solution)/shard_map/all_to_all | solution.py:97
  48.7 12.8 %all-to-all-start.3 = ((bf16[128,4,384]{0,2,1:T(8,128)(2,1)}), bf16[128,4,384]{0,2,1:T(8,128)(2,1)S(1)}, u32[]{:S(2)}, u32[]{:S(2)}) async-start(bf16[128,4,384]{0,2,1:T(8,128)(2,1)} %bitcast.12), calls=%async_computation.3 | async-start | bytes 786432 | tf_op jit(solution)/shard_map/all_to_all | solution.py:99
  53.0 18.6 %copy-start.12 = (f32[4,144,3]{1,0,2:T(4,128)}, f32[4,144,3]{1,0,2:T(4,128)S(1)}, u32[]{:S(2)}) copy-start(f32[4,144,3]{1,0,2:T(4,128)S(1)} %fusion.32) | copy-start | bytes 20740
  53.0 18.6 %copy-start.10 = (f32[4,144,3]{1,0,2:T(4,128)}, f32[4,144,3]{1,0,2:T(4,128)S(1)}, u32[]{:S(2)}) copy-start(f32[4,144,3]{1,0,2:T(4,128)S(1)} %fusion.42) | copy-start | bytes 20740
  53.4 18.2 %copy-start.13 = (f32[576,3]{0,1:T(4,128)}, f32[576,3]{0,1:T(4,128)S(1)}, u32[]{:S(2)}) copy-start(f32[576,3]{0,1:T(4,128)S(1)} %fusion.29) | copy-start | bytes 20740
  61.5 18.4 %all-to-all-start.4 = ((bf16[128,4,384]{0,2,1:T(8,128)(2,1)}), bf16[128,4,384]{0,2,1:T(8,128)(2,1)S(1)}, u32[]{:S(2)}, u32[]{:S(2)}) async-start(bf16[128,4,384]{0,2,1:T(8,128)(2,1)} %bitcast.14), calls=%async_computation.4 | async-start | bytes 786432 | tf_op jit(solution)/shard_map/all_to_all | solution.py:100
  91.6 14.2 %copy-start = (bf16[4,576,3,128]{3,1,2,0:T(8,128)(2,1)S(1)}, bf16[4,576,3,128]{3,1,2,0:T(8,128)(2,1)}, u32[]{:S(2)}) copy-start(bf16[4,576,3,128]{3,1,2,0:T(8,128)(2,1)} %convert_bitcast_fusion) | copy-start | bytes 5308420
  92.8 10.5 %copy-start.14 = (f32[4,144,3]{1,0,2:T(4,128)S(1)}, f32[4,144,3]{1,0,2:T(4,128)}, u32[]{:S(2)}) copy-start(f32[4,144,3]{1,0,2:T(4,128)} %get-tuple-element.63) | copy-start | bytes 20740
  98.4 10.6 %all-to-all-start.10 = ((bf16[4,16,384]{2,1,0:T(8,128)(2,1)}), bf16[4,16,384]{2,1,0:T(8,128)(2,1)S(1)}, u32[]{:S(2)}, u32[]{:S(2)}) async-start(bf16[4,16,384]{2,1,0:T(8,128)(2,1)} %bitcast.44), calls=%async_computation.10 | async-start | bytes 98304 | tf_op jit(solution)/shard_map/all_to_all | solution.py:155
  109.0 9.2 %all-to-all-start.11 = ((bf16[4,16,384]{2,1,0:T(8,128)(2,1)}), bf16[4,16,384]{2,1,0:T(8,128)(2,1)S(1)}, u32[]{:S(2)}, u32[]{:S(2)}) async-start(bf16[4,16,384]{2,1,0:T(8,128)(2,1)} %all_to_all.177), calls=%async_computation.11 | async-start | bytes 98304 | tf_op jit(solution)/shard_map/all_to_all | solution.py:156
  112.5 48.3 %copy-start.19 = (f32[128]{0:T(128)S(1)}, f32[128]{0:T(128)}, u32[]{:S(2)}) copy-start(f32[128]{0:T(128)} %get-tuple-element.60) | copy-start | bytes 1540
  112.5 48.3 %copy-start.20 = (f32[128]{0:T(128)S(1)}, f32[128]{0:T(128)}, u32[]{:S(2)}) copy-start(f32[128]{0:T(128)} %get-tuple-element.62) | copy-start | bytes 1540
  118.2 9.1 %all-to-all-start.9 = ((bf16[4,16,384]{2,1,0:T(8,128)(2,1)}), bf16[4,16,384]{2,1,0:T(8,128)(2,1)S(1)}, u32[]{:S(2)}, u32[]{:S(2)}) async-start(bf16[4,16,384]{2,1,0:T(8,128)(2,1)} %copy_bitcast_fusion), calls=%async_computation.9 | async-start | bytes 98304 | tf_op jit(solution)/shard_map/all_to_all | solution.py:154
  121.5 80.1 %copy-start.9 = (bf16[4,16,384]{2,1,0:T(8,128)(2,1)S(1)}, bf16[4,16,384]{2,1,0:T(8,128)(2,1)}, u32[]{:S(2)}) copy-start(bf16[4,16,384]{2,1,0:T(8,128)(2,1)} %copy-done.8) | copy-start | bytes 147460
  127.2 12.3 %all-to-all-start.7 = ((bf16[4,128,384]{2,1,0:T(8,128)(2,1)}), bf16[4,128,384]{2,1,0:T(8,128)(2,1)S(1)}, u32[]{:S(2)}, u32[]{:S(2)}) async-start(bf16[4,128,384]{2,1,0:T(8,128)(2,1)} %bitcast.38), calls=%async_computation.7 | async-start | bytes 786432 | tf_op jit(solution)/shard_map/all_to_all | solution.py:152
  139.6 17.8 %all-to-all-start.8 = ((bf16[4,128,384]{1,2,0:T(8,128)(2,1)}), bf16[4,128,384]{1,2,0:T(8,128)(2,1)S(1)}, u32[]{:S(2)}, u32[]{:S(2)}) async-start(bf16[4,128,384]{1,2,0:T(8,128)(2,1)} %copy.115), calls=%async_computation.8 | async-start | bytes 786432 | tf_op jit(solution)/shard_map/all_to_all | solution.py:153
  157.4 48.3 %all-to-all-start.6 = ((bf16[4,128,384]{1,2,0:T(8,128)(2,1)}), bf16[4,128,384]{1,2,0:T(8,128)(2,1)S(1)}, u32[]{:S(2)}, u32[]{:S(2)}) async-start(bf16[4,128,384]{1,2,0:T(8,128)(2,1)} %bitcast.27), calls=%async_computation.6 | async-start | bytes 786432 | tf_op jit(solution)/shard_map/all_to_all | solution.py:151
  (11 other events, 27.1 us)
where the time goes:
time: 208 us; the launch traced here: 207 us
  waiting for transfers between devices  53.8 us (26%)
  starting transfers between devices  47.8 us (23%)
  blocking collectives  40.7 us (20%)
  local copies, waits for them, and re-layouts  30.2 us (15%)
  other arithmetic  22.3 us (11%)
  matrix products  10.6 us (5%)
    psum x1, blocking collectives, local(): gain_q, gain_k = lax.psum((dq_gain, dk_gain), ('dp', 'seq'))  40.7 us
    unnamed x53, local copies, waits for them, and re-layouts  11.5 us
    all_to_all x1, waiting for transfers between devices, local(): lax.all_to_all(returned[2], 'seq', split_axis=0, concat_axis=1, tiled=True)  11.2 us
    all_to_all x1, waiting for transfers between devices, local(): lax.all_to_all(image_q, 'seq', split_axis=1, concat_axis=0, tiled=True)  8.56 us
    all_to_all x1, waiting for transfers between devices, local(): lax.all_to_all(returned[1], 'seq', split_axis=0, concat_axis=1, tiled=True)  7.73 us
    reduce_sum x1, other arithmetic, group_back(): log_total = jnp.log(jnp.sum(jnp.exp(shifted), axis=-1, keepdims=True))  7 us
    sub x1, other arithmetic, group_back(): shifted = scores - row_max  6.39 us
    all_to_all x1, starting transfers between devices, local(): lax.all_to_all(text_q, 'seq', split_axis=1, concat_axis=0, tiled=True)  6.35 us
  transfers between devices with their start and end apart: 12, of which 10 were waited for; matrix products, arithmetic and copies ran while one was open for 19% of the time, Pallas kernels for 0%

commit v1 on v0

--- a/solution.py
+++ b/solution.py
@@ -155,7 +155,7 @@
         lax.all_to_all(returned[4], "seq", split_axis=0, concat_axis=1, tiled=True),
         lax.all_to_all(returned[5], "seq", split_axis=0, concat_axis=1, tiled=True),
     )
-    gain_q, gain_k = lax.psum((dq_gain, dk_gain), ("dp", "seq"))
+    gain_q, gain_k = lax.psum(lax.psum((dq_gain, dk_gain), "seq"), "dp")
     return (
         grad_iq[None],
         grad_ik[None],

time: 208 us -> 192 us (0.923)
  blocking collectives: 40.7 us -> 24.4 us
    psum x1 -> x2, blocking collectives: 40.7 us -> 24.4 us  [local(): gain_q, gain_k = lax.psum(lax.psum((dq_gain, dk_gain), 'seq'), 'dp')]
  transfers between devices with their start and end apart: 12 -> 12, of which waited for: 10 -> 10; matrix products, arithmetic and copies ran while one was open for 19% -> 21% of each run, Pallas kernels for 0% -> 0%
where the time goes in v1:
time: 192 us; the launch traced here: 190 us
  waiting for transfers between devices  53.9 us (28%)
  starting transfers between devices  47.8 us (25%)
  local copies, waits for them, and re-layouts  30.2 us (16%)
  blocking collectives  24.4 us (13%)
  other arithmetic  22.3 us (12%)
  matrix products  10.6 us (6%)
    psum x2, blocking collectives, local(): gain_q, gain_k = lax.psum(lax.psum((dq_gain, dk_gain), 'seq'), 'dp')  24.4 us
    unnamed x53, local copies, waits for them, and re-layouts  11.5 us
    all_to_all x1, waiting for transfers between devices, local(): lax.all_to_all(returned[2], 'seq', split_axis=0, concat_axis=1, tiled=True)  11.3 us
    all_to_all x1, waiting for transfers between devices, local(): lax.all_to_all(image_q, 'seq', split_axis=1, concat_axis=0, tiled=True)  8.56 us
    all_to_all x1, waiting for transfers between devices, local(): lax.all_to_all(returned[1], 'seq', split_axis=0, concat_axis=1, tiled=True)  7.73 us
    reduce_sum x1, other arithmetic, group_back(): log_total = jnp.log(jnp.sum(jnp.exp(shifted), axis=-1, keepdims=True))  6.99 us
    sub x1, other arithmetic, group_back(): shifted = scores - row_max  6.4 us
    all_to_all x1, starting transfers between devices, local(): lax.all_to_all(text_q, 'seq', split_axis=1, concat_axis=0, tiled=True)  6.35 us
  transfers between devices with their start and end apart: 12, of which 10 were waited for; matrix products, arithmetic and copies ran while one was open for 21% of the time, Pallas kernels for 0%

profile of v1, /device:TPU:0, one launch (start us, length us, event | category | flops | bytes accessed | tf_op | source)
XLA Modules:
  0.0 190.4 jit_solution(15213148869713327605)
XLA Ops:
  2.2 6.3 %all-to-all-start.2 = ((bf16[16,4,384]{2,0,1:T(8,128)(2,1)}), bf16[16,4,384]{2,0,1:T(8,128)(2,1)S(1)}, u32[]{:S(2)}, u32[]{:S(2)}) async-start(bf16[16,4,384]{2,0,1:T(8,128)(2,1)} %copy.91), calls=%async_computation.2 | async-start | bytes 98304 | tf_op jit(solution)/shard_map/all_to_all | solution.py:101
  9.9 4.3 %all-to-all-done.2 = bf16[16,4,384]{2,0,1:T(8,128)(2,1)S(1)} async-done(((bf16[16,4,384]{2,0,1:T(8,128)(2,1)}), bf16[16,4,384]{2,0,1:T(8,128)(2,1)S(1)}, u32[]{:S(2)}, u32[]{:S(2)}) %all-to-all-start.2) | async-done | bytes 49184 | tf_op jit(solution)/shard_map/all_to_all | solution.py:101
  14.2 3.3 %all-to-all-start.5 = ((bf16[16,4,384]{2,0,1:T(8,128)(2,1)}), bf16[16,4,384]{2,0,1:T(8,128)(2,1)S(1)}, u32[]{:S(2)}, u32[]{:S(2)}) async-start(bf16[16,4,384]{2,0,1:T(8,128)(2,1)} %copy.99), calls=%async_computation.5 | async-start | bytes 98304 | tf_op jit(solution)/shard_map/all_to_all | solution.py:102
  19.4 3.8 %all-to-all-done.5 = bf16[16,4,384]{2,0,1:T(8,128)(2,1)S(1)} async-done(((bf16[16,4,384]{2,0,1:T(8,128)(2,1)}), bf16[16,4,384]{2,0,1:T(8,128)(2,1)S(1)}, u32[]{:S(2)}, u32[]{:S(2)}) %all-to-all-start.5) | async-done | bytes 49184 | tf_op jit(solution)/shard_map/all_to_all | solution.py:102
  23.1 3.5 %all-to-all-start = ((bf16[128,4,384]{0,2,1:T(8,128)(2,1)}), bf16[128,4,384]{0,2,1:T(8,128)(2,1)S(1)}, u32[]{:S(2)}, u32[]{:S(2)}) async-start(bf16[128,4,384]{0,2,1:T(8,128)(2,1)} %bitcast), calls=%async_computation | async-start | bytes 786432 | tf_op jit(solution)/shard_map/all_to_all | solution.py:98
  36.0 3.5 %all-to-all-start.1 = ((bf16[128,4,384]{0,2,1:T(8,128)(2,1)}), bf16[128,4,384]{0,2,1:T(8,128)(2,1)S(1)}, u32[]{:S(2)}, u32[]{:S(2)}) async-start(bf16[128,4,384]{0,2,1:T(8,128)(2,1)} %bitcast.4), calls=%async_computation.1 | async-start | bytes 786432 | tf_op jit(solution)/shard_map/all_to_all | solution.py:97
  40.2 8.6 %all-to-all-done.1 = bf16[128,4,384]{0,2,1:T(8,128)(2,1)S(1)} async-done(((bf16[128,4,384]{0,2,1:T(8,128)(2,1)}), bf16[128,4,384]{0,2,1:T(8,128)(2,1)S(1)}, u32[]{:S(2)}, u32[]{:S(2)}) %all-to-all-start.1) | async-done | bytes 393248 | tf_op jit(solution)/shard_map/all_to_all | solution.py:97
  48.7 3.5 %all-to-all-start.3 = ((bf16[128,4,384]{0,2,1:T(8,128)(2,1)}), bf16[128,4,384]{0,2,1:T(8,128)(2,1)S(1)}, u32[]{:S(2)}, u32[]{:S(2)}) async-start(bf16[128,4,384]{0,2,1:T(8,128)(2,1)} %bitcast.12), calls=%async_computation.3 | async-start | bytes 786432 | tf_op jit(solution)/shard_map/all_to_all | solution.py:99
  57.3 4.2 %all-to-all-done.3 = bf16[128,4,384]{0,2,1:T(8,128)(2,1)S(1)} async-done(((bf16[128,4,384]{0,2,1:T(8,128)(2,1)}), bf16[128,4,384]{0,2,1:T(8,128)(2,1)S(1)}, u32[]{:S(2)}, u32[]{:S(2)}) %all-to-all-start.3) | async-done | bytes 393248 | tf_op jit(solution)/shard_map/all_to_all | solution.py:99
  61.5 3.6 %all-to-all-start.4 = ((bf16[128,4,384]{0,2,1:T(8,128)(2,1)}), bf16[128,4,384]{0,2,1:T(8,128)(2,1)S(1)}, u32[]{:S(2)}, u32[]{:S(2)}) async-start(bf16[128,4,384]{0,2,1:T(8,128)(2,1)} %bitcast.14), calls=%async_computation.4 | async-start | bytes 786432 | tf_op jit(solution)/shard_map/all_to_all | solution.py:100
  65.2 6.4 %bitcast_subtract_fusion = f32[4,3,144,576]{3,2,0,1:T(8,128)} fusion(f32[3,576,4,144]{1,3,2,0:T(8,128)} %bitcast.107), kind=kOutput, calls=%fused_computation.5 | output fusion | flops 2988287 | bytes 7962624 | tf_op jit(solution)/shard_map/while/body/eval_jaxpr/sub | solution.py:30
  73.0 7.0 %fusion.47 = (bf16[4,3,144,576]{3,2,0,1:T(8,128)(2,1)S(1)}, f32[4,3,144,576]{3,2,0,1:T(8,128)}) fusion(f32[4,3,144,576]{3,2,0,1:T(8,128)} %bitcast_subtract_fusion), kind=kOutput, calls=%fused_computation.75 | output fusion | flops 1992959 | bytes 9953280 | tf_op jit(solution)/shard_map/while/body/eval_jaxpr/reduce_sum | solution.py:31
  98.5 4.9 %all-to-all-start.10 = ((bf16[4,16,384]{2,1,0:T(8,128)(2,1)}), bf16[4,16,384]{2,1,0:T(8,128)(2,1)S(1)}, u32[]{:S(2)}, u32[]{:S(2)}) async-start(bf16[4,16,384]{2,1,0:T(8,128)(2,1)} %bitcast.44), calls=%async_computation.10 | async-start | bytes 98304 | tf_op jit(solution)/shard_map/all_to_all | solution.py:155
  109.0 3.5 %all-to-all-start.11 = ((bf16[4,16,384]{2,1,0:T(8,128)(2,1)}), bf16[4,16,384]{2,1,0:T(8,128)(2,1)S(1)}, u32[]{:S(2)}, u32[]{:S(2)}) async-start(bf16[4,16,384]{2,1,0:T(8,128)(2,1)} %all_to_all.177), calls=%async_computation.11 | async-start | bytes 98304 | tf_op jit(solution)/shard_map/all_to_all | solution.py:156
  113.2 5.0 %all-to-all-done.11 = bf16[4,16,384]{2,1,0:T(8,128)(2,1)S(1)} async-done(((bf16[4,16,384]{2,1,0:T(8,128)(2,1)}), bf16[4,16,384]{2,1,0:T(8,128)(2,1)S(1)}, u32[]{:S(2)}, u32[]{:S(2)}) %all-to-all-start.11) | async-done | bytes 49184 | tf_op jit(solution)/shard_map/all_to_all | solution.py:156
  118.2 3.3 %all-to-all-start.9 = ((bf16[4,16,384]{2,1,0:T(8,128)(2,1)}), bf16[4,16,384]{2,1,0:T(8,128)(2,1)S(1)}, u32[]{:S(2)}, u32[]{:S(2)}) async-start(bf16[4,16,384]{2,1,0:T(8,128)(2,1)} %copy_bitcast_fusion), calls=%async_computation.9 | async-start | bytes 98304 | tf_op jit(solution)/shard_map/all_to_all | solution.py:154
  122.5 4.8 %all-to-all-done.9 = bf16[4,16,384]{2,1,0:T(8,128)(2,1)S(1)} async-done(((bf16[4,16,384]{2,1,0:T(8,128)(2,1)}), bf16[4,16,384]{2,1,0:T(8,128)(2,1)S(1)}, u32[]{:S(2)}, u32[]{:S(2)}) %all-to-all-start.9) | async-done | bytes 49184 | tf_op jit(solution)/shard_map/all_to_all | solution.py:154
  127.3 3.5 %all-to-all-start.7 = ((bf16[4,128,384]{2,1,0:T(8,128)(2,1)}), bf16[4,128,384]{2,1,0:T(8,128)(2,1)S(1)}, u32[]{:S(2)}, u32[]{:S(2)}) async-start(bf16[4,128,384]{2,1,0:T(8,128)(2,1)} %bitcast.38), calls=%async_computation.7 | async-start | bytes 786432 | tf_op jit(solution)/shard_map/all_to_all | solution.py:152
  131.9 7.7 %all-to-all-done.7 = bf16[4,128,384]{2,1,0:T(8,128)(2,1)S(1)} async-done(((bf16[4,128,384]{2,1,0:T(8,128)(2,1)}), bf16[4,128,384]{2,1,0:T(8,128)(2,1)S(1)}, u32[]{:S(2)}, u32[]{:S(2)}) %all-to-all-start.7) | async-done | bytes 393248 | tf_op jit(solution)/shard_map/all_to_all | solution.py:152
  139.6 5.6 %all-to-all-start.8 = ((bf16[4,128,384]{1,2,0:T(8,128)(2,1)}), bf16[4,128,384]{1,2,0:T(8,128)(2,1)S(1)}, u32[]{:S(2)}, u32[]{:S(2)}) async-start(bf16[4,128,384]{1,2,0:T(8,128)(2,1)} %copy.115), calls=%async_computation.8 | async-start | bytes 786432 | tf_op jit(solution)/shard_map/all_to_all | solution.py:153
  146.2 11.3 %all-to-all-done.8 = bf16[4,128,384]{1,2,0:T(8,128)(2,1)S(1)} async-done(((bf16[4,128,384]{1,2,0:T(8,128)(2,1)}), bf16[4,128,384]{1,2,0:T(8,128)(2,1)S(1)}, u32[]{:S(2)}, u32[]{:S(2)}) %all-to-all-start.8) | async-done | bytes 393248 | tf_op jit(solution)/shard_map/all_to_all | solution.py:153
  157.5 3.5 %all-to-all-start.6 = ((bf16[4,128,384]{1,2,0:T(8,128)(2,1)}), bf16[4,128,384]{1,2,0:T(8,128)(2,1)S(1)}, u32[]{:S(2)}, u32[]{:S(2)}) async-start(bf16[4,128,384]{1,2,0:T(8,128)(2,1)} %bitcast.27), calls=%async_computation.6 | async-start | bytes 786432 | tf_op jit(solution)/shard_map/all_to_all | solution.py:151
  160.9 12.1 %all-reduce.1 = (f32[128]{0:T(128)S(1)}, f32[128]{0:T(128)S(1)}) all-reduce(f32[128]{0:T(128)S(1)} %copy-done.20, f32[128]{0:T(128)S(1)} %copy-done.19), channel_id=1, replica_groups=mesh['dp'=8,'seq'=4] {'seq'}, use_global_device_ids=true, to_apply=%region_10.11 | all-reduce | flops 256 | bytes 2048 | tf_op jit(solution)/shard_map/psum | solution.py:158
  173.1 12.3 %all-reduce = (f32[128]{0:T(128)}, f32[128]{0:T(128)}) all-reduce(f32[128]{0:T(128)S(1)} %get-tuple-element.66, f32[128]{0:T(128)S(1)} %get-tuple-element.67), channel_id=1, replica_groups=mesh['dp'=8,'seq'=4] {'dp'}, use_global_device_ids=true, to_apply=%region_11.12 | all-reduce | flops 256 | bytes 2048 | tf_op jit(solution)/shard_map/psum | solution.py:158
  (124 shorter events, 54.0 us)
Async XLA Ops:
  0.6 32.1 %copy-start.7 = (bf16[1,128,1536]{2,1,0:T(8,128)(2,1)S(1)}, bf16[1,128,1536]{2,1,0:T(8,128)(2,1)}, u32[]{:S(2)}) copy-start(bf16[1,128,1536]{2,1,0:T(8,128)(2,1)} %param.13) | copy-start | bytes 1179652
  0.6 38.8 %copy-start.15 = (f32[128]{0:T(128)S(1)}, f32[128]{0:T(128)}, u32[]{:S(2)}) copy-start(f32[128]{0:T(128)} %param.19) | copy-start | bytes 1540
  2.2 12.0 %all-to-all-start.2 = ((bf16[16,4,384]{2,0,1:T(8,128)(2,1)}), bf16[16,4,384]{2,0,1:T(8,128)(2,1)S(1)}, u32[]{:S(2)}, u32[]{:S(2)}) async-start(bf16[16,4,384]{2,0,1:T(8,128)(2,1)} %copy.91), calls=%async_computation.2 | async-start | bytes 98304 | tf_op jit(solution)/shard_map/all_to_all | solution.py:101
  14.2 8.9 %all-to-all-start.5 = ((bf16[16,4,384]{2,0,1:T(8,128)(2,1)}), bf16[16,4,384]{2,0,1:T(8,128)(2,1)S(1)}, u32[]{:S(2)}, u32[]{:S(2)}) async-start(bf16[16,4,384]{2,0,1:T(8,128)(2,1)} %copy.99), calls=%async_computation.5 | async-start | bytes 98304 | tf_op jit(solution)/shard_map/all_to_all | solution.py:102
  23.1 12.8 %all-to-all-start = ((bf16[128,4,384]{0,2,1:T(8,128)(2,1)}), bf16[128,4,384]{0,2,1:T(8,128)(2,1)S(1)}, u32[]{:S(2)}, u32[]{:S(2)}) async-start(bf16[128,4,384]{0,2,1:T(8,128)(2,1)} %bitcast), calls=%async_computation | async-start | bytes 786432 | tf_op jit(solution)/shard_map/all_to_all | solution.py:98
  27.5 25.9 %copy-start.17 = (f32[128]{0:T(128)S(1)}, f32[128]{0:T(128)}, u32[]{:S(2)}) copy-start(f32[128]{0:T(128)} %param.18) | copy-start | bytes 1540
  36.0 16.3 %copy-start.3 = (bf16[128,4,384]{0,2,1:T(8,128)(2,1)}, bf16[128,4,384]{0,2,1:T(8,128)(2,1)S(1)}, u32[]{:S(2)}) copy-start(bf16[128,4,384]{0,2,1:T(8,128)(2,1)S(1)} %all-to-all-done) | copy-start | bytes 1179652
  36.0 12.8 %all-to-all-start.1 = ((bf16[128,4,384]{0,2,1:T(8,128)(2,1)}), bf16[128,4,384]{0,2,1:T(8,128)(2,1)S(1)}, u32[]{:S(2)}, u32[]{:S(2)}) async-start(bf16[128,4,384]{0,2,1:T(8,128)(2,1)} %bitcast.4), calls=%async_computation.1 | async-start | bytes 786432 | tf_op jit(solution)/shard_map/all_to_all | solution.py:97
  48.7 12.8 %all-to-all-start.3 = ((bf16[128,4,384]{0,2,1:T(8,128)(2,1)}), bf16[128,4,384]{0,2,1:T(8,128)(2,1)S(1)}, u32[]{:S(2)}, u32[]{:S(2)}) async-start(bf16[128,4,384]{0,2,1:T(8,128)(2,1)} %bitcast.12), calls=%async_computation.3 | async-start | bytes 786432 | tf_op jit(solution)/shard_map/all_to_all | solution.py:99
  53.0 18.6 %copy-start.12 = (f32[4,144,3]{1,0,2:T(4,128)}, f32[4,144,3]{1,0,2:T(4,128)S(1)}, u32[]{:S(2)}) copy-start(f32[4,144,3]{1,0,2:T(4,128)S(1)} %fusion.32) | copy-start | bytes 20740
  53.0 18.6 %copy-start.10 = (f32[4,144,3]{1,0,2:T(4,128)}, f32[4,144,3]{1,0,2:T(4,128)S(1)}, u32[]{:S(2)}) copy-start(f32[4,144,3]{1,0,2:T(4,128)S(1)} %fusion.42) | copy-start | bytes 20740
  53.4 18.2 %copy-start.13 = (f32[576,3]{0,1:T(4,128)}, f32[576,3]{0,1:T(4,128)S(1)}, u32[]{:S(2)}) copy-start(f32[576,3]{0,1:T(4,128)S(1)} %fusion.29) | copy-start | bytes 20740
  61.5 18.4 %all-to-all-start.4 = ((bf16[128,4,384]{0,2,1:T(8,128)(2,1)}), bf16[128,4,384]{0,2,1:T(8,128)(2,1)S(1)}, u32[]{:S(2)}, u32[]{:S(2)}) async-start(bf16[128,4,384]{0,2,1:T(8,128)(2,1)} %bitcast.14), calls=%async_computation.4 | async-start | bytes 786432 | tf_op jit(solution)/shard_map/all_to_all | solution.py:100
  91.6 14.2 %copy-start = (bf16[4,576,3,128]{3,1,2,0:T(8,128)(2,1)S(1)}, bf16[4,576,3,128]{3,1,2,0:T(8,128)(2,1)}, u32[]{:S(2)}) copy-start(bf16[4,576,3,128]{3,1,2,0:T(8,128)(2,1)} %convert_bitcast_fusion) | copy-start | bytes 5308420
  92.8 10.5 %copy-start.14 = (f32[4,144,3]{1,0,2:T(4,128)S(1)}, f32[4,144,3]{1,0,2:T(4,128)}, u32[]{:S(2)}) copy-start(f32[4,144,3]{1,0,2:T(4,128)} %get-tuple-element.63) | copy-start | bytes 20740
  98.5 10.6 %all-to-all-start.10 = ((bf16[4,16,384]{2,1,0:T(8,128)(2,1)}), bf16[4,16,384]{2,1,0:T(8,128)(2,1)S(1)}, u32[]{:S(2)}, u32[]{:S(2)}) async-start(bf16[4,16,384]{2,1,0:T(8,128)(2,1)} %bitcast.44), calls=%async_computation.10 | async-start | bytes 98304 | tf_op jit(solution)/shard_map/all_to_all | solution.py:155
  109.0 9.2 %all-to-all-start.11 = ((bf16[4,16,384]{2,1,0:T(8,128)(2,1)}), bf16[4,16,384]{2,1,0:T(8,128)(2,1)S(1)}, u32[]{:S(2)}, u32[]{:S(2)}) async-start(bf16[4,16,384]{2,1,0:T(8,128)(2,1)} %all_to_all.177), calls=%async_computation.11 | async-start | bytes 98304 | tf_op jit(solution)/shard_map/all_to_all | solution.py:156
  112.5 48.4 %copy-start.19 = (f32[128]{0:T(128)S(1)}, f32[128]{0:T(128)}, u32[]{:S(2)}) copy-start(f32[128]{0:T(128)} %get-tuple-element.60) | copy-start | bytes 1540
  112.6 48.4 %copy-start.20 = (f32[128]{0:T(128)S(1)}, f32[128]{0:T(128)}, u32[]{:S(2)}) copy-start(f32[128]{0:T(128)} %get-tuple-element.62) | copy-start | bytes 1540
  118.2 9.1 %all-to-all-start.9 = ((bf16[4,16,384]{2,1,0:T(8,128)(2,1)}), bf16[4,16,384]{2,1,0:T(8,128)(2,1)S(1)}, u32[]{:S(2)}, u32[]{:S(2)}) async-start(bf16[4,16,384]{2,1,0:T(8,128)(2,1)} %copy_bitcast_fusion), calls=%async_computation.9 | async-start | bytes 98304 | tf_op jit(solution)/shard_map/all_to_all | solution.py:154
  121.5 63.9 %copy-start.9 = (bf16[4,16,384]{2,1,0:T(8,128)(2,1)S(1)}, bf16[4,16,384]{2,1,0:T(8,128)(2,1)}, u32[]{:S(2)}) copy-start(bf16[4,16,384]{2,1,0:T(8,128)(2,1)} %copy-done.8) | copy-start | bytes 147460
  127.3 12.3 %all-to-all-start.7 = ((bf16[4,128,384]{2,1,0:T(8,128)(2,1)}), bf16[4,128,384]{2,1,0:T(8,128)(2,1)S(1)}, u32[]{:S(2)}, u32[]{:S(2)}) async-start(bf16[4,128,384]{2,1,0:T(8,128)(2,1)} %bitcast.38), calls=%async_computation.7 | async-start | bytes 786432 | tf_op jit(solution)/shard_map/all_to_all | solution.py:152
  139.6 17.9 %all-to-all-start.8 = ((bf16[4,128,384]{1,2,0:T(8,128)(2,1)}), bf16[4,128,384]{1,2,0:T(8,128)(2,1)S(1)}, u32[]{:S(2)}, u32[]{:S(2)}) async-start(bf16[4,128,384]{1,2,0:T(8,128)(2,1)} %copy.115), calls=%async_computation.8 | async-start | bytes 786432 | tf_op jit(solution)/shard_map/all_to_all | solution.py:153
  157.5 32.0 %all-to-all-start.6 = ((bf16[4,128,384]{1,2,0:T(8,128)(2,1)}), bf16[4,128,384]{1,2,0:T(8,128)(2,1)S(1)}, u32[]{:S(2)}, u32[]{:S(2)}) async-start(bf16[4,128,384]{1,2,0:T(8,128)(2,1)} %bitcast.27), calls=%async_computation.6 | async-start | bytes 786432 | tf_op jit(solution)/shard_map/all_to_all | solution.py:151
  (11 other events, 27.1 us)
